TPU v7x, 32 devices: a whole 2x2x4 slice. The times are simulated.
32 devices in a mesh: rep: 1, r: 8 (over y, z), s: 4 (over x, core).
Axes of the slice: x: 2, y: 2, z: 4, core: 2. Of those that a mesh axis runs over, the one named last changes fastest.
Arguments:
- x: bfloat16 [32, 4096, 640], P(('rep', 'r', 's'))
- dy: bfloat16 [32, 4096, 640], P(('rep', 'r', 's'))
- w_gate: bfloat16 [2, 640, 2432], P(None, 's')
- w_up: bfloat16 [2, 640, 2432], P(None, 's')
- w_down: bfloat16 [2, 2432, 640], P(None, 's')
- m_w_gate: float32 [2, 640, 2432], P(None, 's')
- m_w_up: float32 [2, 640, 2432], P(None, 's')
- m_w_down: float32 [2, 2432, 640], P(None, 's')
- v_w_gate: float32 [2, 640, 2432], P(None, 's')
- v_w_up: float32 [2, 640, 2432], P(None, 's')
- v_w_down: float32 [2, 2432, 640], P(None, 's')
Outputs:
- output 1: bfloat16 [2, 640, 2432], P('rep', 's')
- output 2: bfloat16 [2, 640, 2432], P('rep', 's')
- output 3: bfloat16 [2, 2432, 640], P('rep', 's')
- output 4: float32 [2, 640, 2432], P('rep', 's')
- output 5: float32 [2, 640, 2432], P('rep', 's')
- output 6: float32 [2, 2432, 640], P('rep', 's')
- output 7: float32 [2, 640, 2432], P('rep', 's')
- output 8: float32 [2, 640, 2432], P('rep', 's')
- output 9: float32 [2, 2432, 640], P('rep', 's')
All inputs are finite; a program needn't handle non-finite values.
Results may differ from a plain program's by a relative error of at most 0.022.
Values are sent between devices in bfloat16 or wider.
A program may use at most 2 GiB of HBM per device.

v0:
```python
import jax
import jax.numpy as jnp
from jax import lax
from jax.sharding import PartitionSpec as P

NAMES = ("w_gate", "w_up", "w_down")


def matmul(a, w):
    return jnp.dot(a, w, preferred_element_type=jnp.float32).astype(jnp.bfloat16)


def normed(h):
    wide = h.astype(jnp.float32)
    scale = lax.rsqrt(jnp.mean(wide**2, -1, keepdims=True) + 1e-6)
    return (wide * scale).astype(jnp.bfloat16)


def layer(h, w):
    a = normed(h)
    gate = jnp.dot(a, w["w_gate"], preferred_element_type=jnp.float32)
    up = jnp.dot(a, w["w_up"], preferred_element_type=jnp.float32)
    return h + matmul((jax.nn.silu(gate) * up).astype(jnp.bfloat16), w["w_down"])


def adamw(w, m, v, g):
    m = 0.9 * m + 0.1 * g
    v = 0.95 * v + 0.05 * g * g
    step = m * lax.rsqrt(v + 1e-8) + 0.1 * w
    return (w - 0.02 * step).astype(jnp.bfloat16), m, v


def clipped(gradients, sum_of_squares, count):
    factor = jnp.minimum(1.0, 0.5 * lax.rsqrt(sum_of_squares / count + 1e-30))
    return [g * factor for g in gradients]


def solution(mesh):
    def fetched(weights, number):
        return {name: lax.all_gather(w[number], "s", axis=0, tiled=True) for name, w in zip(NAMES, weights, strict=True)}

    def summed(term):
        return lax.psum(lax.psum_scatter(term, "s", scatter_dimension=0, tiled=True), "r")

    def step(x, dy, *arrays):
        weights, m, v = (arrays[i : i + 3] for i in (0, 3, 6))
        layers = weights[0].shape[0]
        h, kept = x[0], []
        for number in range(layers):
            kept.append(h)
            h = layer(h, fetched(weights, number))
        by_h, mine = dy[0], [None] * layers
        for number in reversed(range(layers)):
            _, back = jax.vjp(lambda w, h: layer(h, w), fetched(weights, number), kept[number])
            by_w, by_h = back(by_h)
            mine[number] = [summed(by_w[name]) for name in NAMES]
        gradients = [jnp.stack([mine[number][i] for number in range(layers)]).astype(jnp.float32) for i in range(3)]
        squares = lax.psum(sum(jnp.sum(g * g) for g in gradients), "s")
        gradients = clipped(gradients, squares, lax.psum(1, "s") * sum(g.size for g in gradients))
        new = [adamw(w.astype(jnp.float32), m, v, g) for w, m, v, g in zip(weights, m, v, gradients, strict=True)]
        return tuple(one[which] for which in range(3) for one in new)

    states, cut = P(("rep", "r", "s"), None, None), P(None, "s", None)
    return jax.shard_map(
        step,
        mesh=mesh,
        in_specs=(states, states) + (cut,) * 9,
        out_specs=(P("rep", "s", None),) * 9,
        check_vma=False,
    )
```

profile of v0, /device:TPU:0, one launch (start us, length us, event | category | flops | bytes accessed | tf_op | source)
XLA Modules:
  0.0 784.7 jit_solution(5050462748921465293)
XLA Ops:
  7.2 2.7 fusion.93
  10.0 0.0 all-gather.15.cloned.1.call-start
  10.0 2.6 fusion.92
  12.7 0.0 all-gather.17.cloned.1.call-start
  12.7 1.3 fusion.91
  14.1 0.5 all-gather.23.cloned.1.call-update
  14.6 0.5 all-gather.21.cloned.1.call-update
  15.2 0.5 all-gather.19.cloned.1.call-update
  15.8 8.0 %copy.20 = bf16[1,4096,640]{1,2,0:T(8,128)(2,1)} copy(bf16[1,4096,640]{2,1,0:T(8,128)(2,1)} %param.11) | data formatting | bytes 10485760 | tf_op args[0]
  23.8 3.6 fusion.15
  27.4 8.0 %copy.21 = bf16[1,4096,640]{1,2,0:T(8,128)(2,1)} copy(bf16[1,4096,640]{2,1,0:T(8,128)(2,1)} %param.12) | data formatting | bytes 10485760 | tf_op args[1]
  35.4 5.5 all-gather.13.cloned.1.call-done
  41.0 26.0 %fusion.50 = f32[4096,2432]{1,0:T(8,128)} fusion(bf16[1,4096,640]{1,2,0:T(8,128)(2,1)} %copy.20, f32[4096]{0:T(1024)S(1)} %add_rsqrt_fusion, bf16[1,640,2432]{2,1,0:T(8,128)(2,1)} %all-gather.13.cloned.1.call-done), kind=kOutput, calls=%fused_computation.75 | convolution fusion | flops 12758548480 | bytes 48218112 | tf_op jit(solution)/shard_map/dot_general | solution.py:21
  67.0 4.2 all-gather.15.cloned.1.call-done
  71.2 39.7 %multiply_convert_fusion.1 = (bf16[4096,2432]{1,0:T(8,128)(2,1)}, f32[4096,2432]{1,0:T(8,128)}) fusion(f32[4096,2432]{1,0:T(8,128)} %fusion.50, bf16[1,640,2432]{2,1,0:T(8,128)(2,1)} %all-gather.15.cloned.1.call-done, bf16[1,4096,640]{1,2,0:T(8,128)(2,1)} %copy.20, f32[4096]{0:T(1024)S(1)} %add_rsqrt_fusion), kind=kOutput, calls=%fused_computation.17 | convolution fusion | flops 12818317312 | bytes 107986944 | tf_op jit(solution)/shard_map/dot_general | solution.py:22
  110.9 22.1 %fusion.19 = (f32[4096]{0:T(1024)S(1)}, bf16[4096,640]{0,1:T(8,128)(2,1)}) fusion(bf16[4096,2432]{1,0:T(8,128)(2,1)} %get-tuple-element.30, bf16[1,2432,640]{2,1,0:T(8,128)(2,1)} %all-gather.17.cloned.1.call-done, bf16[1,4096,640]{1,2,0:T(8,128)(2,1)} %copy.20), kind=kOutput, calls=%fused_computation.37 | convolution fusion | flops 12763787264 | bytes 33538048 | tf_op jit(solution)/shard_map/dot_general | solution.py:10
  133.0 0.6 copy-done.14
  133.7 26.4 %fusion.42 = f32[4096,2432]{1,0:T(8,128)} fusion(bf16[4096,640]{0,1:T(8,128)(2,1)} %get-tuple-element.33, f32[4096]{0:T(1024)S(1)} %fusion.79, bf16[1,640,2432]{2,1,0:T(8,128)(2,1)} %all-gather.23.cloned.1.call-done), kind=kOutput, calls=%fused_computation.72 | convolution fusion | flops 12758548480 | bytes 48218112 | tf_op jit(solution)/shard_map/jvp()/dot_general | solution.py:22
  160.1 1.5 all-gather.21.cloned.1.call-done
  161.5 22.4 %convolution_convert_fusion.1 = bf16[4096,2432]{1,0:T(8,128)(2,1)} fusion(bf16[1,4096,640]{2,1,0:T(8,128)(2,1)} %param.12, bf16[1,2432,640]{2,1,0:T(8,128)(2,1)} %all-gather.21.cloned.1.call-done), kind=kOutput, calls=%fused_computation.23 | convolution fusion | flops 12760645632 | bytes 28278784 | tf_op jit(solution)/shard_map/transpose(jvp())/dot_general | solution.py:10
  183.9 7.7 all-gather.19.cloned.1.call-done
  191.6 53.6 %fusion.2 = (bf16[4096,2432]{1,0:T(8,128)(2,1)}, f32[4096,2432]{1,0:T(8,128)}) fusion(f32[4096,2432]{1,0:T(8,128)} %fusion.42, bf16[4096,2432]{1,0:T(8,128)(2,1)} %convolution_convert_fusion.1, bf16[1,640,2432]{2,1,0:T(8,128)(2,1)} %all-gather.19.cloned.1.call-done, bf16[4096,640]{0,1:T(8,128)(2,1)} %get-tuple-element.33, f32[4096]{0:T(1024)S(1)} %fusion.79), kind=kOutput, calls=%fused_computation.8 | convolution fusion | flops 12878086144 | bytes 127909888 | tf_op jit(solution)/shard_map/jvp()/dot_general | solution.py:21
  245.1 26.3 %fusion.23 = bf16[4096,640]{0,1:T(8,128)(2,1)} fusion(bf16[4096,2432]{1,0:T(8,128)(2,1)} %convolution_convert_fusion.1, bf16[1,640,2432]{2,1,0:T(8,128)(2,1)S(1)} %copy-done.19, f32[4096,2432]{1,0:T(8,128)} %get-tuple-element.35), kind=kOutput, calls=%fused_computation.41 | convolution fusion | flops 12813074432 | bytes 68124672 | tf_op jit(solution)/shard_map/transpose(jvp())/dot_general | solution.py:22
  271.5 23.3 %fusion.21 = (f32[4096]{0:T(1024)S(1)}, bf16[4096,640]{0,1:T(8,128)(2,1)}) fusion(bf16[4096,640]{0,1:T(8,128)(2,1)} %get-tuple-element.33, bf16[4096,640]{0,1:T(8,128)(2,1)} %fusion.23, bf16[4096,2432]{1,0:T(8,128)(2,1)} %get-tuple-element.34, bf16[1,640,2432]{2,1,0:T(8,128)(2,1)} %all-gather.19.cloned.1.call-done), kind=kOutput, calls=%fused_computation.39 | convolution fusion | flops 12763787264 | bytes 38780928 | tf_op jit(solution)/shard_map/transpose(jvp())/dot_general | solution.py:21
  294.9 11.9 %fusion.26 = bf16[4096,640]{0,1:T(8,128)(2,1)} fusion(bf16[4096,640]{0,1:T(8,128)(2,1)} %get-tuple-element.33, bf16[4096,640]{0,1:T(8,128)(2,1)} %get-tuple-element.37, bf16[1,4096,640]{1,2,0:T(8,128)(2,1)} %copy.21, f32[4096]{0:T(1024)S(1)} %multiply_multiply_fusion.3, f32[4096]{0:T(1024)S(1)} %fusion.79), kind=kLoop, calls=%fused_computation.45 | loop fusion | flops 18350080 | bytes 21004288 | tf_op jit(solution)/shard_map/transpose(jvp())/add_any | solution.py:14
  306.8 22.0 %convolution_convert_fusion.4 = bf16[2432,640]{1,0:T(8,128)(2,1)} fusion(bf16[4096,2432]{1,0:T(8,128)(2,1)} %get-tuple-element.30, bf16[4096,640]{0,1:T(8,128)(2,1)} %fusion.26), kind=kOutput, calls=%fused_computation.51 | convolution fusion | flops 12752240640 | bytes 28278784 | tf_op jit(solution)/shard_map/transpose(jvp())/dot_general | solution.py:10
  328.9 31.8 %fusion.34 = bf16[2432,640]{1,0:T(8,128)(2,1)} fusion(bf16[1,4096,640]{2,1,0:T(8,128)(2,1)} %param.12, f32[4096,2432]{1,0:T(8,128)} %fusion.42, f32[4096,2432]{1,0:T(8,128)} %get-tuple-element.35), kind=kOutput, calls=%fused_computation.52 | convolution fusion | flops 12812009472 | bytes 88047616 | tf_op jit(solution)/shard_map/transpose(jvp())/dot_general | solution.py:10
  360.8 22.0 %convolution_convert_fusion = bf16[4096,2432]{1,0:T(8,128)(2,1)} fusion(bf16[4096,640]{0,1:T(8,128)(2,1)} %fusion.26, bf16[1,2432,640]{2,1,0:T(8,128)(2,1)S(1)} %copy-done.18), kind=kOutput, calls=%fused_computation.22 | convolution fusion | flops 12760645632 | bytes 28278784 | tf_op jit(solution)/shard_map/transpose(jvp())/dot_general | solution.py:10
  382.8 28.6 %fusion.33 = bf16[640,2432]{1,0:T(8,128)(2,1)} fusion(bf16[4096,2432]{1,0:T(8,128)(2,1)} %convolution_convert_fusion, f32[4096,2432]{1,0:T(8,128)} %fusion.50, bf16[1,4096,640]{1,2,0:T(8,128)(2,1)} %copy.20, f32[4096]{0:T(1024)S(1)} %copy-done.17), kind=kOutput, calls=%fused_computation.50 | convolution fusion | flops 12819873792 | bytes 68141056 | tf_op jit(solution)/shard_map/transpose(jvp())/dot_general | solution.py:22
  411.5 28.9 %fusion.29 = bf16[640,2432]{1,0:T(8,128)(2,1)} fusion(bf16[4096,2432]{1,0:T(8,128)(2,1)} %convolution_convert_fusion.1, bf16[4096,640]{0,1:T(8,128)(2,1)} %get-tuple-element.33, f32[4096]{0:T(1024)S(1)} %copy-done.13, f32[4096,2432]{1,0:T(8,128)} %get-tuple-element.35), kind=kOutput, calls=%fused_computation.48 | convolution fusion | flops 12819873792 | bytes 68141056 | tf_op jit(solution)/shard_map/transpose(jvp())/dot_general | solution.py:22
  440.5 0.0 reduce-scatter.7.cloned.1.call-start
  440.5 37.6 %fusion.30 = bf16[640,2432]{1,0:T(8,128)(2,1)} fusion(f32[4096,2432]{1,0:T(8,128)} %fusion.50, f32[4096,2432]{1,0:T(8,128)} %get-tuple-element.31, bf16[4096,2432]{1,0:T(8,128)(2,1)} %convolution_convert_fusion, bf16[1,4096,640]{1,2,0:T(8,128)(2,1)} %copy.20, f32[4096]{0:T(1024)S(1)} %copy-done.17), kind=kOutput, calls=%fused_computation.49 | convolution fusion | flops 12869681152 | bytes 107986944 | tf_op jit(solution)/shard_map/transpose(jvp())/dot_general | solution.py:21
  478.2 0.0 reduce-scatter.9.cloned.1.call-start
  478.2 20.7 %convolution_convert_fusion.5 = bf16[640,2432]{1,0:T(8,128)(2,1)} fusion(bf16[4096,2432]{1,0:T(8,128)(2,1)} %get-tuple-element.34, bf16[4096,640]{0,1:T(8,128)(2,1)} %get-tuple-element.33, f32[4096]{0:T(1024)S(1)} %copy-done.13), kind=kOutput, calls=%fused_computation.53 | convolution fusion | flops 12758548480 | bytes 28295168 | tf_op jit(solution)/shard_map/transpose(jvp())/dot_general | solution.py:21
  499.1 30.5 %reduce-scatter.7.cloned.1.call-done = bf16[160,2432]{1,0:T(8,128)(2,1)} async-done(((bf16[640,2432]{1,0:T(8,128)(2,1)}), bf16[160,2432]{1,0:T(8,128)(2,1)}) %reduce-scatter.7.cloned.1.call-update) | async-done | bytes 778256 | tf_op jit(solution)/shard_map/reduce_scatter | solution.py:43
  529.6 40.3 %reduce-scatter.9.cloned.1.call-done = bf16[160,2432]{1,0:T(8,128)(2,1)} async-done(((bf16[640,2432]{1,0:T(8,128)(2,1)}), bf16[160,2432]{1,0:T(8,128)(2,1)}) %reduce-scatter.9.cloned.1.call-update) | async-done | bytes 778256 | tf_op jit(solution)/shard_map/reduce_scatter | solution.py:43
  569.9 171.9 %all-reduce.3.cloned.1.call-done = (bf16[1,160,2432]{2,1,0:T(8,128)(2,1)}, bf16[1,160,2432]{2,1,0:T(8,128)(2,1)}, bf16[1,160,2432]{2,1,0:T(8,128)(2,1)}, bf16[1,...) async-done(((bf16[1,160,2432]{2,1,0:T(8,128)(2,1)}, bf16[1,160,2432]{2,1,0:T(8,128)(2,1)}, bf16[1,160,2432]{2,1,0:T(8,128)(2,1)}, ...) | async-done | bytes 4669456 | tf_op jit(solution)/shard_map/psum | solution.py:43
  741.8 2.8 fusion.60
  744.6 2.8 fusion.59
  747.3 2.9 fusion.58
  752.2 6.7 psum.55
  759.6 7.1 fusion.66
  766.7 1.6 copy-done.5
  768.3 0.9 copy-done.6
  769.2 0.9 copy-done.7
  770.1 0.1 copy-done.8
  770.2 0.2 copy-done.9
  770.4 7.3 fusion.57
  (62 shorter events, 0.8 us)
Async XLA Ops:
  7.2 5.5 copy-start
  7.2 33.8 %all-gather.13.cloned.1.call-start = ((), (), s32[]{:S(2)}) async-start(), calls=%async_computation.12 | async-start | bytes 3891200 | tf_op jit(solution)/shard_map/all_gather | solution.py:40
  10.0 61.2 %all-gather.15.cloned.1.call-start = ((), (), s32[]{:S(2)}) async-start(), calls=%async_computation.13 | async-start | bytes 3891200 | tf_op jit(solution)/shard_map/all_gather | solution.py:40
  12.7 98.2 %all-gather.17.cloned.1.call-start = ((), (), s32[]{:S(2)}) async-start(), calls=%async_computation.14 | async-start | bytes 3891200 | tf_op jit(solution)/shard_map/all_gather | solution.py:40
  14.0 119.7 %all-gather.23.cloned.1.call-start = ((), (), s32[]{:S(2)}) async-start(), calls=%async_computation.17 | async-start | bytes 3891200 | tf_op jit(solution)/shard_map/all_gather | solution.py:40
  14.6 146.9 %all-gather.21.cloned.1.call-start = ((), (), s32[]{:S(2)}) async-start(), calls=%async_computation.16 | async-start | bytes 3891200 | tf_op jit(solution)/shard_map/all_gather | solution.py:40
  15.2 176.4 %all-gather.19.cloned.1.call-start = ((), (), s32[]{:S(2)}) async-start(), calls=%async_computation.15 | async-start | bytes 3891200 | tf_op jit(solution)/shard_map/all_gather | solution.py:40
  15.8 483.3 %reduce-scatter.15.cloned.1.call-start = ((), (), s32[]{:S(2)}) async-start(), calls=%async_computation.10 | async-start | bytes 3891200 | tf_op jit(solution)/shard_map/reduce_scatter | solution.py:43
  27.4 43.8 %copy-start.16 = (f32[4096]{0:T(1024)}, f32[4096]{0:T(1024)S(1)}, u32[]{:S(2)}) copy-start(f32[4096]{0:T(1024)S(1)} %add_rsqrt_fusion) | copy-start | bytes 49156
  133.0 0.6 copy-start.14
  133.6 161.2 %copy-start.12 = (f32[4096]{0:T(1024)}, f32[4096]{0:T(1024)S(1)}, u32[]{:S(2)}) copy-start(f32[4096]{0:T(1024)S(1)} %fusion.79) | copy-start | bytes 49156
  183.9 61.2 %copy-start.19 = (bf16[1,640,2432]{2,1,0:T(8,128)(2,1)S(1)}, bf16[1,640,2432]{2,1,0:T(8,128)(2,1)}, u32[]{:S(2)}) copy-start(bf16[1,640,2432]{2,1,0:T(8,128)(2,1)} %all-gather.23.cloned.1.call-done) | copy-start | bytes 9338884
  271.5 23.4 %copy-start.15 = (f32[4096]{0:T(1024)S(1)}, f32[4096]{0:T(1024)}, u32[]{:S(2)}) copy-start(f32[4096]{0:T(1024)} %copy-done.14) | copy-start | bytes 49156
  328.8 31.9 %copy-start.18 = (bf16[1,2432,640]{2,1,0:T(8,128)(2,1)S(1)}, bf16[1,2432,640]{2,1,0:T(8,128)(2,1)}, u32[]{:S(2)}) copy-start(bf16[1,2432,640]{2,1,0:T(8,128)(2,1)} %all-gather.17.cloned.1.call-done) | copy-start | bytes 9338884
  328.8 170.2 %reduce-scatter.17.cloned.1.call-start = ((), (), s32[]{:S(2)}) async-start(), calls=%async_computation.11 | async-start | bytes 3891200 | tf_op jit(solution)/shard_map/reduce_scatter | solution.py:43
  360.7 22.1 %copy-start.17 = (f32[4096]{0:T(1024)S(1)}, f32[4096]{0:T(1024)}, u32[]{:S(2)}) copy-start(f32[4096]{0:T(1024)} %copy-done.16) | copy-start | bytes 49156
  360.7 138.4 %reduce-scatter.11.cloned.1.call-start = ((), (), s32[]{:S(2)}) async-start(), calls=%async_computation.8 | async-start | bytes 3891200 | tf_op jit(solution)/shard_map/reduce_scatter | solution.py:43
  382.8 28.7 %copy-start.13 = (f32[4096]{0:T(1024)S(1)}, f32[4096]{0:T(1024)}, u32[]{:S(2)}) copy-start(f32[4096]{0:T(1024)} %copy-done.12) | copy-start | bytes 49156
  411.4 87.7 %reduce-scatter.13.cloned.1.call-start = ((), (), s32[]{:S(2)}) async-start(), calls=%async_computation.9 | async-start | bytes 3891200 | tf_op jit(solution)/shard_map/reduce_scatter | solution.py:43
  440.5 89.1 %reduce-scatter.7.cloned.1.call-start = ((), (), s32[]{:S(2)}) async-start(), calls=%async_computation.6 | async-start | bytes 3891200 | tf_op jit(solution)/shard_map/reduce_scatter | solution.py:43
  478.2 91.7 %reduce-scatter.9.cloned.1.call-start = ((), (), s32[]{:S(2)}) async-start(), calls=%async_computation.7 | async-start | bytes 3891200 | tf_op jit(solution)/shard_map/reduce_scatter | solution.py:43
  499.0 260.6 %copy-start.1 = (bf16[2,608,640]{2,1,0:T(8,128)(2,1)S(1)}, bf16[2,608,640]{2,1,0:T(8,128)(2,1)}, u32[]{:S(2)}) copy-start(bf16[2,608,640]{2,1,0:T(8,128)(2,1)} %param.15) | copy-start | bytes 4669444
  499.0 242.8 %all-reduce.3.cloned.1.call-start = ((), (), s32[]{:S(2)}) async-start(), calls=%async_computation.18 | async-start | bytes 9338880 | tf_op jit(solution)/shard_map/psum | solution.py:43
  747.3 19.4 %copy-start.10 = (bf16[1,160,2432]{2,1,0:T(8,128)(2,1)S(1)}, bf16[1,160,2432]{2,1,0:T(8,128)(2,1)}, u32[]{:S(2)}) copy-start(bf16[1,160,2432]{2,1,0:T(8,128)(2,1)} %get-tuple-element.11) | copy-start | bytes 2334724
  747.3 19.4 %copy-start.11 = (bf16[1,160,2432]{2,1,0:T(8,128)(2,1)S(1)}, bf16[1,160,2432]{2,1,0:T(8,128)(2,1)}, u32[]{:S(2)}) copy-start(bf16[1,160,2432]{2,1,0:T(8,128)(2,1)} %get-tuple-element.12) | copy-start | bytes 2334724
  759.5 7.2 copy-start.2
  759.5 7.2 copy-start.3
  759.5 7.2 copy-start.4
  759.6 8.7 %copy-start.5 = (f32[2,160,2432]{2,1,0:T(8,128)S(1)}, f32[2,160,2432]{2,1,0:T(8,128)}, u32[]{:S(2)}) copy-start(f32[2,160,2432]{2,1,0:T(8,128)} %param.16) | copy-start | bytes 9338884
  759.6 9.6 %copy-start.6 = (f32[2,160,2432]{2,1,0:T(8,128)S(1)}, f32[2,160,2432]{2,1,0:T(8,128)}, u32[]{:S(2)}) copy-start(f32[2,160,2432]{2,1,0:T(8,128)} %param.20) | copy-start | bytes 9338884
  759.6 10.5 %copy-start.7 = (f32[2,160,2432]{2,1,0:T(8,128)S(1)}, f32[2,160,2432]{2,1,0:T(8,128)}, u32[]{:S(2)}) copy-start(f32[2,160,2432]{2,1,0:T(8,128)} %param.17) | copy-start | bytes 9338884
  759.6 10.6 %copy-start.8 = (bf16[1,160,2432]{2,1,0:T(8,128)(2,1)S(1)}, bf16[1,160,2432]{2,1,0:T(8,128)(2,1)}, u32[]{:S(2)}) copy-start(bf16[1,160,2432]{2,1,0:T(8,128)(2,1)} %get-tuple-element.9) | copy-start | bytes 2334724
  759.6 10.8 %copy-start.9 = (bf16[1,160,2432]{2,1,0:T(8,128)(2,1)S(1)}, bf16[1,160,2432]{2,1,0:T(8,128)(2,1)}, u32[]{:S(2)}) copy-start(bf16[1,160,2432]{2,1,0:T(8,128)(2,1)} %get-tuple-element.10) | copy-start | bytes 2334724
Sparse Core Ops, SparseCore 0:
  10.1 30.7 all-gather.12
  43.1 28.0 all-gather.14
  73.3 28.0 all-gather.16
  103.4 28.0 all-gather.22
  133.4 28.0 all-gather.20
  163.5 28.0 all-gather.18
  329.0 37.2 reduce-scatter.14
  369.4 37.2 reduce-scatter.16
  411.6 37.2 reduce-scatter.10
  451.9 37.2 reduce-scatter.12
  492.3 37.2 reduce-scatter.6
  532.6 37.2 reduce-scatter.8
  574.3 167.4 all-reduce.2
where the time goes:
time: 793 us; the launch traced here: 785 us
  matrix products  432 us (54%)
  waiting for transfers between devices  263 us (33%)
  other arithmetic  38.4 us (5%)
  local copies, waits for them, and re-layouts  27 us (3%)
  between operations  17.3 us (2%)
    psum x1, waiting for transfers between devices, summed(): lax.psum(lax.psum_scatter(term, 's', scatter_dimension=0, tiled=True), 'r')  172 us
    dot_general x5, matrix products, layer(): gate = jnp.dot(a, w['w_gate'], preferred_element_type=jnp.float32)  161 us
    dot_general x5, matrix products, layer(): up = jnp.dot(a, w['w_up'], preferred_element_type=jnp.float32)  150 us
    dot_general x5, matrix products, matmul(): jnp.dot(a, w, preferred_element_type=jnp.float32).astype(jnp.bfloat16)  120 us
    reduce_scatter x6, waiting for transfers between devices, summed(): lax.psum_scatter(term, 's', scatter_dimension=0, tiled=True)  70.8 us
    unnamed x42, local copies, waits for them, and re-layouts  20.4 us
    all_gather x6, waiting for transfers between devices, fetched(): lax.all_gather(w[number], 's', axis=0, tiled=True)  18.9 us
  transfers between devices with their start and end apart: 13, of which 7 were waited for; matrix products, arithmetic and copies ran while one was open for 42% of the time, Pallas kernels for 0%

commit v1 on v0

v1 whole, which is shorter than its diff:
```python
import functools

import jax
import jax.numpy as jnp
from jax import lax
from jax.experimental import pallas as pl
from jax.experimental.pallas import tpu as pltpu
from jax.sharding import PartitionSpec as P

F32, BF16 = jnp.float32, jnp.bfloat16
TILE = 512
VMEM_LIMIT = 62 * 1024 * 1024


def dot(a, b, ca=1, cb=0):
    return lax.dot_general(a, b, (((ca,), (cb,)), ((), ())), preferred_element_type=F32)


def cuts(n, size=256):
    return [(i, min(size, n - i)) for i in range(0, n, size)]


def params(*semantics):
    return pltpu.CompilerParams(dimension_semantics=semantics, vmem_limit_bytes=VMEM_LIMIT)


def rows(tile, width):
    return pl.BlockSpec((tile, width), lambda i: (i, 0))


def whole(*shape):
    return pl.BlockSpec(shape, lambda i: (0,) * len(shape))


def sds(shape, dtype):
    return jax.ShapeDtypeStruct(shape, dtype)


def cost(flops, nbytes):
    return pl.CostEstimate(flops=int(flops), bytes_accessed=int(nbytes), transcendentals=0)


def norm_of(h):
    wide = h.astype(F32)
    scale = lax.rsqrt(jnp.mean(wide * wide, -1, keepdims=True) + 1e-6)
    return (wide * scale).astype(BF16)


def silu_parts(g):
    sig = jax.nn.sigmoid(g)
    return sig, g * sig


def once(*shape):
    return pl.BlockSpec(shape, lambda i: (0,) * len(shape), pipeline_mode=pl.Buffered(1))


ANY = pl.BlockSpec(memory_space=pl.ANY)
MESH = pl.DeviceIdType.MESH
DMA = pltpu.SemaphoreType.DMA
ZS = 4


class Place:
    def __init__(self):
        r, s = lax.axis_index("r"), lax.axis_index("s")
        self.y, z, self.x, self.c = r // ZS, r % ZS, s // 2, s % 2
        self.za = ((z + 1) // 2) % 2
        self.ids = {
            "c": (0, r, 2 * self.x + 1 - self.c),
            "x": (0, r, 2 * (1 - self.x) + self.c),
            "y": (0, (1 - self.y) * ZS + z, s),
            "za": (0, self.y * ZS + z + 1 - 2 * (z % 2), s),
            "zb": (0, self.y * ZS + ZS - 1 - z, s),
        }

    def greet(self, names):
        barrier = pltpu.get_barrier_semaphore()
        for name in names:
            pl.semaphore_signal(barrier, inc=1, device_id=self.ids[name], device_id_type=MESH)
        pl.semaphore_wait(barrier, len(names))

    def copy(self, src, dst, send, recv, to):
        return pltpu.make_async_remote_copy(
            src_ref=src, dst_ref=dst, send_sem=send, recv_sem=recv, device_id=self.ids[to], device_id_type=MESH
        )


class Gather:
    def __init__(self, place, src, full, send, recv, local):
        n = src.shape[0]
        h = n // 2
        p = place
        own, far = 2 * p.x + p.c, 2 * (1 - p.x) + p.c

        def at(block, y, size):
            return full.at[pl.ds(pl.multiple_of(block * n + y * h, 16), size)]

        self.local = pltpu.make_async_copy(src, at(own, 0, n), local)
        self.x = p.copy(src.at[pl.ds(pl.multiple_of(p.y * h, 16), h)], at(own, p.y, h), send.at[0], recv.at[0], "x")
        self.y = p.copy(at(far, p.y, h), at(far, p.y, h), send.at[1], recv.at[1], "y")
        self.co = p.copy(src, at(own, 0, n), send.at[2], recv.at[2], "c")
        self.ca = p.copy(at(far, p.y, h), at(far, p.y, h), send.at[3], recv.at[3], "c")
        self.cb = p.copy(at(far, 1 - p.y, h), at(far, 1 - p.y, h), send.at[4], recv.at[4], "c")

    def start(self):
        self.x.start()
        self.co.start()
        self.local.start()

    def middle(self):
        self.x.wait_recv()
        self.y.start()
        self.ca.start()

    def last(self):
        self.y.wait_recv()
        self.cb.start()

    def finish(self):
        self.local.wait()
        for one in (self.co, self.ca, self.cb):
            one.wait_recv()
        for one in (self.x, self.y, self.co, self.ca, self.cb):
            one.wait_send()


def forward_body(x_ref, wg_ref, wu_ref, wd_ref, a_ref, g_ref, u_ref, h_ref, a1_ref, d0_ref, g1_ref, u1_ref, d1_ref, *scratch):
    fulls, (z_ref, send, recv, local) = scratch[:6], scratch[6:]
    i = pl.program_id(0)
    place = Place()
    blocks = [w.at[layer] for layer in range(2) for w in (wg_ref, wu_ref, wd_ref)]
    gathers = [Gather(place, blocks[k], fulls[k], send.at[k], recv.at[k], local.at[k]) for k in range(6)]

    @pl.when(i == 0)
    def _():
        place.greet("cxy")
        for one in gathers[:3]:
            one.start()
        for one in gathers[:3]:
            one.middle()
        for one in gathers[:3]:
            one.last()
        for one in gathers[:3]:
            one.finish()
        for one in gathers[3:]:
            one.start()

    for k in range(3):

        @pl.when(i == 3 + 3 * k)
        def _(one=gathers[3 + k]):
            one.middle()

        @pl.when(i == 6 + 3 * k)
        def _(one=gathers[3 + k]):
            one.last()

    a = norm_of(x_ref[...])
    a_ref[...] = a
    for at, n in cuts(z_ref.shape[1]):
        at = slice(at, at + n)
        g = dot(a, fulls[0][:, at])
        u = dot(a, fulls[1][:, at])
        g_ref[:, at] = g
        u_ref[:, at] = u
        z_ref[:, at] = (silu_parts(g)[1] * u).astype(BF16)
    h = (x_ref[...].astype(F32) + dot(z_ref[...], fulls[2][...]).astype(BF16).astype(F32)).astype(BF16)
    h_ref[...] = h
    a1_ref[...] = norm_of(h)

    @pl.when(i == pl.num_programs(0) - 1)
    def _():
        for one in gathers[3:]:
            one.finish()
        outs = [pltpu.make_async_copy(fulls[2 + k], out, local.at[k]) for k, out in enumerate((d0_ref, g1_ref, u1_ref, d1_ref))]
        for one in outs:
            one.start()
        for one in outs:
            one.wait()


def forward(x, wg, wu, wd):
    t, d = x.shape
    f = wg.shape[2]
    tile = 256
    mats = [(d, f), (d, f), (f, d)] * 2
    return pl.pallas_call(
        forward_body,
        grid=(t // tile,),
        in_specs=[rows(tile, d), ANY, ANY, ANY],
        out_specs=[rows(tile, d), rows(tile, f), rows(tile, f), rows(tile, d), rows(tile, d)] + [ANY] * 4,
        out_shape=[sds((t, d), BF16), sds((t, f), F32), sds((t, f), F32), sds((t, d), BF16), sds((t, d), BF16)]
        + [sds(one, BF16) for one in mats[2:]],
        scratch_shapes=[pltpu.VMEM(one, BF16) for one in mats] + [pltpu.VMEM((tile, f), BF16), DMA((6, 5)), DMA((6, 5)), DMA((6,))],
        compiler_params=pltpu.CompilerParams(
            dimension_semantics=("arbitrary",), vmem_limit_bytes=VMEM_LIMIT, collective_id=0, has_side_effects=True
        ),
        cost_estimate=cost(6 * t * d * f, 12 * t * f),
        name="forward",
    )(x, wg, wu, wd)


class Sum:
    def __init__(self, place, term, out, squares, buffers, sems):
        self.p, self.term, self.out, self.squares = place, term, out, squares
        self.rc, self.rx, self.sx, self.keep, self.ry, self.ra, self.rb, self.fin, self.temp = buffers
        send, recv, self.local = sems
        p = place
        self.ka, self.kx = [], None
        for x in range(2):
            self.ka.append(p.copy(term.at[pl.ds(4 * (2 * x + 1 - p.c), 4)], self.rc.at[x], send.at[x], recv.at[x], "c"))
        self.cx = p.copy(self.sx, self.rx, send.at[2], recv.at[2], "x")
        two, one, last = self.sx.at[pl.ds(0, 2)], self.sx.at[2], self.sx.at[3]
        self.cy = p.copy(two, self.ry, send.at[3], recv.at[3], "y")
        self.cza = p.copy(one, self.ra, send.at[4], recv.at[4], "za")
        self.czb = p.copy(last, self.rb, send.at[5], recv.at[5], "zb")
        self.at = 2 * p.y + p.za
        mine = self.fin.at[self.at]
        self.back = p.copy(mine, mine, send.at[6], recv.at[6], "za")
        half = self.fin.at[pl.ds(2 * p.y, 2)]
        self.wide = p.copy(half, half, send.at[7], recv.at[7], "y")
        self.done = pltpu.make_async_copy(self.fin, out, self.local.at[0])

    def a(self):
        for one in self.ka:
            one.start()

    def b(self):
        p = self.p
        for one in self.ka:
            one.wait_recv()
        loads = []
        for k, x in enumerate((1 - p.x, p.x)):
            loads.append(pltpu.make_async_copy(self.term.at[pl.ds(4 * (2 * x + p.c), 4)], self.temp.at[2 * k], self.local.at[2 * k]))
            loads.append(pltpu.make_async_copy(self.rc.at[x], self.temp.at[2 * k + 1], self.local.at[2 * k + 1]))
        for one in loads:
            one.start()
        for one in loads[:2]:
            one.wait()
        for q in range(4):
            self.sx[q] = (self.temp[0, q].astype(F32) + self.temp[1, q].astype(F32)).astype(BF16)
        self.cx.start()
        for one in loads[2:]:
            one.wait()
        for q in range(4):
            self.keep[q] = self.temp[2, q].astype(F32) + self.temp[3, q].astype(F32)

    def c_(self):
        self.cx.wait()
        load = pltpu.make_async_copy(self.rx, self.temp.at[0], self.local.at[0])
        load.start()
        load.wait()
        p = self.p
        for q in range(2):
            at = 2 * (1 - p.y) + q
            self.sx[q] = (self.keep[at] + self.temp[0, at].astype(F32)).astype(BF16)
        self.cy.start()
        for q in range(2):
            at = 2 * p.y + q
            self.keep[at] = self.keep[at] + self.temp[0, at].astype(F32)

    def d(self):
        self.cy.wait_recv()
        p = self.p
        self.sx[2] = (self.keep[2 * p.y + 1 - p.za] + self.ry[1 - p.za].astype(F32)).astype(BF16)
        self.cza.start()
        self.keep[self.at] = self.keep[self.at] + self.ry[p.za].astype(F32)

    def e(self):
        self.cza.wait_recv()
        self.sx[3] = (self.keep[self.at] + self.ra[...].astype(F32)).astype(BF16)
        self.czb.start()

    def f(self):
        self.czb.wait_recv()
        piece = (self.sx[3].astype(F32) + self.rb[...].astype(F32)).astype(BF16)
        self.fin[self.at] = piece
        self.back.start()
        wide = piece.astype(F32)
        self.squares[0, 0] += jnp.sum(wide * wide)

    def g(self):
        self.back.wait_recv()
        self.wide.start()

    def h(self):
        self.wide.wait_recv()
        self.done.start()

    def finish(self):
        for one in self.ka + [self.cy, self.cza, self.czb, self.back, self.wide]:
            one.wait_send()
        self.done.wait()


def quarters(shape):
    return (16, shape[0] // 16, shape[1])


def sum_scratch(shape):
    _, a, b = shape
    return [
        pltpu.VMEM((4, a, b), BF16),
        pltpu.VMEM((4, a, b), F32),
        pltpu.VMEM((2, a, b), BF16),
        pltpu.VMEM((a, b), BF16),
        pltpu.VMEM((a, b), BF16),
        pltpu.VMEM((4, a, b), BF16),
    ]


def landing(shape):
    return [sds((2, 4) + shape[1:], BF16), sds((4,) + shape[1:], BF16)]


def kept_out(shape):
    return sds((4,) + shape[1:], BF16)


def split_up(at, per, refs, count=3):
    return [refs[at + k * per : at + (k + 1) * per] for k in range(count)]


def make_sums(place, terms, outs, squares, lands, own, temps, sems):
    send, recv, local = sems
    return [
        Sum(
            place,
            terms[k],
            outs[k],
            squares,
            (lands[k][0], lands[k][1], own[k][0], own[k][1], own[k][2], own[k][3], own[k][4], own[k][5], temps[terms[k].shape[2]]),
            (send.at[k], recv.at[k], local.at[k]),
        )
        for k in range(len(terms))
    ]


NEAR = ("c", "x", "y", "za", "zb")


def algebra(g, u, dz):
    sig, act = silu_parts(g)
    z = (act * u).astype(BF16)
    dz = dz.astype(BF16).astype(F32)
    du = (dz * act).astype(BF16)
    dg = (dz * u * (sig + act * (1.0 - sig))).astype(BF16)
    return z, dg, du


def store_turned(out, acc):
    n = out.shape[1]
    for at in range(0, acc.shape[1], 128):
        block = acc[:, at : at + 128].T.astype(BF16)
        row = at
        while row < at + 128:
            k, r = row // n, row % n
            more = min(n - r, at + 128 - row)
            out[k, r : r + more, :] = block[row - at : row - at + more, :]
            row += more


def store_quarters(out, acc):
    n = out.shape[1]
    for k in range(out.shape[0]):
        out[k] = acc[k * n : (k + 1) * n, :].astype(BF16)


def hidden_body(a_ref, dy_ref, wg_ref, wu_ref, wd_ref, dg_ref, du_ref, dwd_ref, acc):
    i = pl.program_id(0)

    @pl.when(i == 0)
    def _():
        acc[...] = jnp.zeros_like(acc)

    a, dy = a_ref[...], dy_ref[...]
    across = dy.T
    for at, n in cuts(acc.shape[1]):
        at = slice(at, at + n)
        g, u = dot(a, wg_ref[:, at]), dot(a, wu_ref[:, at])
        z, dg, du = algebra(g, u, dot(dy, wd_ref[at, :], 1, 1))
        dg_ref[:, at] = dg
        du_ref[:, at] = du
        acc[:, at] += dot(across, z)

    @pl.when(i == pl.num_programs(0) - 1)
    def _():
        store_turned(dwd_ref, acc)


def hidden(a, dy, wg, wu, wd):
    t, d = dy.shape
    f = wd.shape[0]
    tile = 512
    shape = quarters((f, d))
    return pl.pallas_call(
        hidden_body,
        grid=(t // tile,),
        in_specs=[rows(tile, d), rows(tile, d), once(d, f), once(d, f), once(f, d)],
        out_specs=[rows(tile, f), rows(tile, f), once(*shape)],
        out_shape=[sds((t, f), BF16), sds((t, f), BF16), sds(shape, BF16)],
        scratch_shapes=[pltpu.VMEM((d, f), F32)],
        compiler_params=params("arbitrary"),
        cost_estimate=cost(8 * t * d * f, 12 * t * f),
        name="hidden",
    )(a, dy, wg, wu, wd)


def grads_body(a_ref, c_ref, e_ref, out_c, out_e, acc_c, acc_e):
    i = pl.program_id(0)

    @pl.when(i == 0)
    def _():
        acc_c[...] = jnp.zeros_like(acc_c)
        acc_e[...] = jnp.zeros_like(acc_e)

    across = a_ref[...].T
    for acc, ref in ((acc_c, c_ref), (acc_e, e_ref)):
        for at, n in cuts(ref.shape[1]):
            at = slice(at, at + n)
            acc[:, at] += dot(across, ref[:, at])

    @pl.when(i == pl.num_programs(0) - 1)
    def _():
        store_quarters(out_c, acc_c)
        store_quarters(out_e, acc_e)


def grads(a, c, e):
    (t, d), f = a.shape, c.shape[1]
    tile = 512
    shape = quarters((d, f))
    return pl.pallas_call(
        grads_body,
        grid=(t // tile,),
        in_specs=[rows(tile, d), rows(tile, f), rows(tile, f)],
        out_specs=[once(*shape)] * 2,
        out_shape=[sds(shape, BF16)] * 2,
        scratch_shapes=[pltpu.VMEM((d, f), F32)] * 2,
        compiler_params=params("arbitrary"),
        cost_estimate=cost(4 * t * d * f, 4 * t * f),
        name="grads",
    )(a, c, e)


def back_body(dg1, du1, h_ref, dy_ref, g_ref, u_ref, wg_ref, wu_ref, wd_ref, *refs):
    terms, refs = refs[:3], refs[3:]
    dg_ref, du_ref, dwd_ref, sq_ref = refs[:4]
    outs, lands, refs = refs[4:7], [refs[7:9], refs[9:11], refs[11:13]], refs[13:]
    acc, own, refs = refs[0], split_up(1, 6, refs), refs[19:]
    temps = {terms[0].shape[2]: refs[0], terms[2].shape[2]: refs[1]}
    i = pl.program_id(0)
    place = Place()
    sums = make_sums(place, terms, outs, sq_ref, lands, own, temps, refs[2:5])

    @pl.when(i == 0)
    def _():
        place.greet(NEAR)
        sq_ref[0, 0] = 0.0
        for k in (2, 0, 1):
            sums[k].a()
        acc[...] = jnp.zeros_like(acc)

    plan = {1: ("b2", "b0", "b1"), 4: ("c2",), 6: ("d2", "c0"), 7: ("e2",), 8: ("d0", "f2", "c1"), 9: ("e0",), 10: ("g2", "d1", "f0"), 11: ("e1",), 12: ("h2", "g0", "f1"), 13: ("g1",), 14: ("h0",), 15: ("h1",)}
    for at, what in plan.items():

        @pl.when(i == at)
        def _(what=what):
            for one in what:
                stage(sums, one)

    da = dot(dg1[...], wg_ref[...], 1, 1) + dot(du1[...], wu_ref[...], 1, 1)
    da = da.astype(BF16).astype(F32)
    h = h_ref[...].astype(F32)
    count = h.shape[-1]
    scale = lax.rsqrt(jnp.sum(h * h, -1, keepdims=True) / count + 1e-6)
    inner = jnp.sum(da * h, -1, keepdims=True) / count
    dh = da * scale - h * (inner * (scale * scale * scale))
    dh = (dy_ref[...].astype(F32) + dh.astype(BF16).astype(F32)).astype(BF16)
    across = dh.T
    for at, n in cuts(acc.shape[1]):
        at = slice(at, at + n)
        z, dg, du = algebra(g_ref[:, at], u_ref[:, at], dot(dh, wd_ref[at, :], 1, 1))
        dg_ref[:, at] = dg
        du_ref[:, at] = du
        acc[:, at] += dot(across, z)

    @pl.when(i == pl.num_programs(0) - 1)
    def _():
        store_turned(dwd_ref, acc)
        for one in sums:
            one.finish()


def stage(sums, what):
    one = sums[int(what[1])]
    {"a": one.a, "b": one.b, "c": one.c_, "d": one.d, "e": one.e, "f": one.f, "g": one.g, "h": one.h}[what[0]]()


def sum_outs(shapes):
    kinds = [kept_out(one) for one in shapes]
    for one in shapes:
        kinds += landing(one)
    return kinds


def sum_own(shapes):
    out = []
    for one in shapes:
        out += sum_scratch(one)
    for one in dict.fromkeys(shapes):
        out.append(pltpu.VMEM((4, 4) + one[1:], BF16))
    n = len(shapes)
    return out + [DMA((n, 8)), DMA((n, 8)), DMA((n, 4))]


def back(dg1, du1, h, dy, g0, u0, wg, wu, wd, terms):
    t, d = h.shape
    f = wd.shape[0]
    tile = 256
    shapes = [one.shape for one in terms]
    out = quarters((f, d))
    kinds = sum_outs(shapes)
    results = pl.pallas_call(
        back_body,
        grid=(t // tile,),
        in_specs=[rows(tile, f), rows(tile, f), rows(tile, d), rows(tile, d), rows(tile, f), rows(tile, f)]
        + [once(d, f), once(d, f), once(f, d)]
        + [ANY] * 3,
        out_specs=[rows(tile, f), rows(tile, f), once(*out), pl.BlockSpec(memory_space=pltpu.SMEM)] + [ANY] * len(kinds),
        out_shape=[sds((t, f), BF16), sds((t, f), BF16), sds(out, BF16), sds((1, 1), F32)] + kinds,
        scratch_shapes=[pltpu.VMEM((d, f), F32)] + sum_own(shapes),
        compiler_params=pltpu.CompilerParams(
            dimension_semantics=("arbitrary",), vmem_limit_bytes=67043328, collective_id=1, has_side_effects=True
        ),
        cost_estimate=cost(8 * t * d * f, 12 * t * f),
        name="back",
    )(dg1, du1, h, dy, g0, u0, wg, wu, wd, *terms)
    return results[:3], results[3], results[4:7]


def tail_body(a_ref, c_ref, e_ref, term_d, sq1_ref, *refs):
    tot_ref, outs, lands, refs = refs[0], refs[1:5], split_up(5, 2, refs, 4), refs[13:]
    sq_ref, acc, made, own, refs = refs[0], refs[1], refs[2:5], split_up(5, 6, refs, 4), refs[29:]
    terms = (*made, term_d)
    temps = {one.shape[2]: refs[k] for k, one in enumerate(terms)}
    tot_in, tot_send, tot_recv = refs[7:10]
    i = pl.program_id(0)
    n = pl.num_programs(0) // 3
    cut = made[1].shape[2]
    place = Place()
    sums = make_sums(place, terms, outs, sq_ref, lands, own, temps, refs[4:7])

    @pl.when(i == 0)
    def _():
        place.greet(NEAR)
        sq_ref[0, 0] = sq1_ref[0, 0]
        sums[3].a()

    @pl.when((i == 0) | (i == n))
    def _():
        acc[...] = jnp.zeros_like(acc)

    plan = {1: ("b3",), 4: ("b0",), 5: ("c3",), 8: ("b1", "d3"), 9: ("c0", "e3"), 10: ("f3",), 11: ("g3", "d0")}
    for at, what in plan.items():

        @pl.when(i == at)
        def _(what=what):
            for one in what:
                stage(sums, one)

    def add(ref, lo, hi):
        across = a_ref[...].T
        for at in range(lo, hi, 256):
            at = slice(at, min(at + 256, hi))
            acc[:, at] += dot(across, ref[:, at])

    for k, (ref, lo, hi) in enumerate(((c_ref, 0, c_ref.shape[1]), (e_ref, 0, cut), (e_ref, cut, c_ref.shape[1]))):

        @pl.when((i >= k * n) & (i < (k + 1) * n))
        def _(ref=ref, lo=lo, hi=hi):
            add(ref, lo, hi)

        @pl.when(i == (k + 1) * n - 1)
        def _(k=k, lo=lo, hi=hi):
            rows_each = made[k].shape[1]
            for q in range(16):
                made[k][q] = acc[q * rows_each : (q + 1) * rows_each, lo:hi].astype(BF16)
            sums[k].a()

    @pl.when(i == pl.num_programs(0) - 1)
    def _():
        for one in ("b2", "e0", "c1", "h3", "f0", "d1", "c2", "g0", "e1", "d2", "f1", "e2", "g1", "f2"):
            stage(sums, one)
        tot_ref[...] = jnp.full(tot_ref.shape, sq_ref[0, 0], F32)
        for k, name in enumerate(("c", "x", "y", "za")):
            if k == 1:
                sums[2].g()
            one = place.copy(tot_ref, tot_in.at[k], tot_send.at[k], tot_recv.at[k], name)
            one.start()
            one.wait()
            tot_ref[...] = tot_ref[...] + tot_in[k]
        for one in ("h0", "h1", "h2"):
            stage(sums, one)
        for one in sums:
            one.finish()


def tail(a, c, e, term_d, squares):
    (t, d), f = a.shape, c.shape[1]
    tile = 1024
    n = t // tile
    cut = f // 256 // 2 * 256 + 256
    made = quarters((d, f))
    shapes = [made, made[:2] + (cut,), made[:2] + (f - cut,), term_d.shape]
    kinds = sum_outs(shapes)
    smem = pl.BlockSpec(memory_space=pltpu.SMEM)
    results = pl.pallas_call(
        tail_body,
        grid=(3 * n,),
        in_specs=[
            pl.BlockSpec((tile, d), lambda i: (i % n, 0)),
            pl.BlockSpec((tile, f), lambda i: (jnp.minimum(i, n - 1), 0)),
            pl.BlockSpec((tile, f), lambda i: (jnp.where(i < n, 0, i % n), 0)),
            ANY,
            smem,
        ],
        out_specs=[pl.BlockSpec((8, 128), lambda i: (0, 0))] + [ANY] * len(kinds),
        out_shape=[sds((8, 128), F32)] + kinds,
        scratch_shapes=[pltpu.SMEM((1, 1), F32), pltpu.VMEM((d, f), F32)]
        + [pltpu.VMEM(one, BF16) for one in shapes[:3]]
        + sum_own(shapes)
        + [pltpu.VMEM((4, 8, 128), F32), DMA((4,)), DMA((4,))],
        compiler_params=pltpu.CompilerParams(
            dimension_semantics=("arbitrary",), vmem_limit_bytes=67043328, collective_id=2, has_side_effects=True
        ),
        cost_estimate=cost(4 * t * d * f, 4 * t * f),
        name="tail",
    )(a, c, e, term_d, squares)
    return results[0][0, 0], results[1:5]


def solution(mesh):
    def step(x, dy, *arrays):
        x, dy = x[0], dy[0]
        weights, m, v = (arrays[i : i + 3] for i in (0, 3, 6))
        a0, g0, u0, h1, a1, wd0, wg1, wu1, wd1 = forward(x, *weights)
        dg1, du1, d_wd1 = hidden(a1, dy, wg1, wu1, wd1)
        d_wg1, d_wu1 = grads(a1, dg1, du1)
        (dg0, du0, d_wd0), squares1, sums1 = back(dg1, du1, h1, dy, g0, u0, wg1, wu1, wd0, (d_wg1, d_wu1, d_wd1))
        squares, (s_g, s_ua, s_ub, s_d) = tail(a0, dg0, du0, d_wd0, squares1)
        sums0 = (s_g, jnp.concatenate([s_ua, s_ub], -1), s_d)
        count = 4 * sum(w.size for w in weights)
        factor = jnp.minimum(1.0, 0.5 * lax.rsqrt(squares / count + 1e-30))
        new = []
        for i in range(3):
            g = jnp.stack([sums0[i], sums1[i]]).reshape(weights[i].shape).astype(F32) * factor
            w = weights[i].astype(F32)
            mi = 0.9 * m[i] + 0.1 * g
            vi = 0.95 * v[i] + 0.05 * g * g
            new.append(((w - 0.02 * (mi * lax.rsqrt(vi + 1e-8) + 0.1 * w)).astype(BF16), mi, vi))
        return tuple(one[which] for which in range(3) for one in new)

    states, cut = P(("rep", "r", "s"), None, None), P(None, "s", None)
    return jax.shard_map(
        step,
        mesh=mesh,
        in_specs=(states, states) + (cut,) * 9,
        out_specs=(P("rep", "s", None),) * 9,
        check_vma=False,
    )
```

time: 793 us -> 503 us (0.63)
  Pallas kernels: 0 us -> 471 us
  matrix products: 432 us -> 0 us
  waiting for transfers between devices: 263 us -> 0 us
  other arithmetic: 38.4 us -> 15.8 us
  local copies, waits for them, and re-layouts: 27 us -> 5.15 us
  between operations: 17.3 us -> 1.83 us
    pallas_call x0 -> x5, Pallas kernels: none -> 471 us  [the longest x1 127 us: back(): pl.pallas_call(back_body, grid=(t // tile,), in_specs=[rows(tile, f), row...]
    dot_general x15 -> x0, matrix products: 432 us -> none  [the longest x5 161 us: layer(): gate = jnp.dot(a, w['w_gate'], preferred_element_type=jnp.float32)]
    psum x1 -> x0, waiting for transfers between devices: 172 us -> none  [summed(): lax.psum(lax.psum_scatter(term, 's', scatter_dimension=0, tiled=True), 'r')]
    reduce_scatter x6 -> x0, waiting for transfers between devices: 70.8 us -> none  [summed(): lax.psum_scatter(term, 's', scatter_dimension=0, tiled=True)]
    all_gather x6 -> x0, waiting for transfers between devices: 18.9 us -> none  [fetched(): lax.all_gather(w[number], 's', axis=0, tiled=True)]
    unnamed x42 -> x18, local copies, waits for them, and re-layouts: 20.4 us -> 3.95 us
    reduce_sum x4 -> x0, other arithmetic: 12 us -> none  [the longest x3 8.42 us: step(): squares = lax.psum(sum((jnp.sum(g * g) for g in gradients)), 's')]
    add_any x1 -> x0, other arithmetic: 11.9 us -> none  [normed(): wide = h.astype(jnp.float32)]
  transfers between devices with their start and end apart: 13 -> 0, of which waited for: 7 -> 0; matrix products, arithmetic and copies ran while one was open for 42% -> 0% of each run, Pallas kernels for 0% -> 0%
where the time goes in v1:
time: 503 us; the launch traced here: 494 us
  Pallas kernels  471 us (94%)
  other arithmetic  15.8 us (3%)
  local copies, waits for them, and re-layouts  5.15 us (1%)
    pallas_call x1, Pallas kernels, back(): pl.pallas_call(back_body, grid=(t // tile,), in_specs=[rows(tile, f), row...  127 us
    pallas_call x1, Pallas kernels, tail(): pl.pallas_call(tail_body, grid=(3 * n,), in_specs=[pl.BlockSpec((tile, d)...  114 us
    pallas_call x1, Pallas kernels, forward(): pl.pallas_call(forward_body, grid=(t // tile,), in_specs=[rows(tile, d),...  107 us
    pallas_call x1, Pallas kernels, hidden(): pl.pallas_call(hidden_body, grid=(t // tile,), in_specs=[rows(tile, d), r...  78.3 us
    pallas_call x1, Pallas kernels, grads(): pl.pallas_call(grads_body, grid=(t // tile,), in_specs=[rows(tile, d), ro...  44.7 us
    convert_element_type x2, other arithmetic, step(): (w - 0.02 * (mi * lax.rsqrt(vi + 1e-08) + 0.1 * w)).astype(BF16)  14.6 us

profile of v1, /device:TPU:0, one launch (start us, length us, event | category | flops | bytes accessed | tf_op | source)
XLA Modules:
  0.0 493.8 jit_solution(4593248172186673162)
XLA Ops:
  0.6 106.9 %forward.1 = (bf16[4096,640]{1,0:T(8,128)(2,1)}, f32[4096,2432]{1,0:T(8,128)}, f32[4096,2432]{1,0:T(8,128)}, bf16[4096,640]{1,0:T(8,128)(2,1)}, bf16[4096,640]{1...) custom-call(bf16[4096,640]{1,0:T(8,128)(2,1)} %bitcast.15, ...), custom_call_target="tpu_custom_call" | custom-call | flops 38252052480 | bytes 119537664 | tf_op jit(solution)/shard_map/forward/pallas_call | solution.py:188
  107.5 78.3 %hidden.1 = (bf16[4096,2432]{1,0:T(8,128)(2,1)}, bf16[4096,2432]{1,0:T(8,128)(2,1)}, bf16[16,152,640]{2,1,0:T(8,128)(2,1)}) custom-call(bf16[4096,640]{1,0:T(8,128)(2,1)} %get-tuple-element.36.a_ref, bf16[4096,640]{1,0:T(8,128)(2,1)} %bitcast.16, bf16[640,2432]{1,0:T(8,128)(2,1)} %get-tuple-element.37.wg_ref, bf16[640,2432]{1,0:T(8,128)(2,1)} %get-tuple-element.38.wu_ref, ...), custom_call_target="tpu_custom_call" | custom-call | flops 51002736640 | bytes 119537664 | tf_op jit(solution)/shard_map/hidden/pallas_call | solution.py:397
  185.8 44.7 %grads.1 = (bf16[16,40,2432]{2,1,0:T(8,128)(2,1)}, bf16[16,40,2432]{2,1,0:T(8,128)(2,1)}) custom-call(bf16[4096,640]{1,0:T(8,128)(2,1)} %get-tuple-element.36.a_ref, bf16[4096,2432]{1,0:T(8,128)(2,1)} %get-tuple-element.40.c_ref.dg1, bf16[4096,2432]{1,0:T(8,128)(2,1)} %get-tuple-element.41.e_ref.du1), custom_call_target="tpu_custom_call" | custom-call | flops 25501368320 | bytes 39845888 | tf_op jit(solution)/shard_map/grads/pallas_call | solution.py:434
  230.6 127.2 %back.1 = (bf16[4096,2432]{1,0:T(8,128)(2,1)}, bf16[4096,2432]{1,0:T(8,128)(2,1)}, bf16[16,152,640]{2,1,0:T(8,128)(2,1)}, f32[1,1]{1,0:T(1,128)}, bf16[4,40,2432...) custom-call(bf16[4096,2432]{1,0:T(8,128)(2,1)} %get-tuple-element.40, ...), custom_call_target="tpu_custom_call" | custom-call | flops 51002736640 | bytes 119537664 | tf_op jit(solution)/shard_map/back/pallas_call | solution.py:525
  357.7 113.9 %tail.1 = (f32[8,128]{1,0:T(8,128)}, bf16[4,40,2432]{2,1,0:T(8,128)(2,1)}, bf16[4,40,1280]{2,1,0:T(8,128)(2,1)}, bf16[4,40,1152]{2,1,0:T(8,128)(2,1)}, bf16[4,15...) custom-call(bf16[4096,640]{1,0:T(8,128)(2,1)} %get-tuple-element.35., ...), custom_call_target="tpu_custom_call" | custom-call | flops 25501368320 | bytes 39845888 | tf_op jit(solution)/shard_map/tail/pallas_call | solution.py:619
  471.7 1.2 slice.3
  473.6 0.0 copy-start.8
  473.6 1.2 pad_maximum_fusion.3
  474.8 0.0 copy-start
  474.9 0.0 copy-start.1
  474.9 0.0 copy-start.2
  474.9 0.0 copy-start.3
  474.9 0.0 copy-start.4
  474.9 0.0 copy-start.5
  474.9 0.0 copy-start.6
  474.9 0.0 copy-start.7
  474.9 7.3 %fusion.8 = (bf16[2,608,640]{2,1,0:T(8,128)(2,1)}, f32[2,608,640]{2,1,0:T(8,128)}, f32[2,608,640]{2,1,0:T(8,128)}) fusion(bf16[2,608,640]{2,1,0:T(8,128)(2,1)} %wd_ref.1, f32[]{:T(128)} %bitcast.4, bf16[1,608,640]{2,1,0:T(8,128)(2,1)} %bitcast.12, bf16[1,608,640]{2,1,0:T(8,128)(2,1)} %bitcast.14, f32[2,608,640]{2,1,0:T(8,128)} %param.21, ...), kind=kLoop, calls=%fused_computation.17 | loop fusion | flops 15564800 | bytes 17121284 | tf_op jit(solution)/shard_map/convert_element_type | solution.py:662
  482.2 0.0 copy-done.8
  482.2 0.0 copy-done
  482.2 0.8 copy-done.1
  483.0 1.1 copy-done.2
  484.1 0.9 copy-done.3
  485.0 0.4 copy-done.4
  485.3 0.4 copy-done.5
  485.8 0.2 copy-done.6
  485.9 0.2 copy-done.7
  486.2 7.3 %fusion.2 = (bf16[2,160,2432]{2,1,0:T(8,128)(2,1)}, f32[2,160,2432]{2,1,0:T(8,128)}, f32[2,160,2432]{2,1,0:T(8,128)}, bf16[2,160,2432]{2,1,0:T(8,128)(2,1)}, f32...) fusion(bf16[2,160,2432]{2,1,0:T(8,128)(2,1)S(1)} %copy-done.4, f32[]{:T(128)} %bitcast.4, ...), kind=kLoop, calls=%fused_computation.11 | loop fusion | flops 31129600 | bytes 34242564 | tf_op jit(solution)/shard_map/convert_element_type | solution.py:662
Async XLA Ops:
  473.6 8.7 %copy-start.8 = (bf16[4,40,2432]{2,1,0:T(8,128)(2,1)S(1)}, bf16[4,40,2432]{2,1,0:T(8,128)(2,1)}, u32[]{:S(2)}) copy-start(bf16[4,40,2432]{2,1,0:T(8,128)(2,1)} %get-tuple-element.53) | copy-start | bytes 2334724
  474.8 7.4 %copy-start = (f32[2,160,2432]{2,1,0:T(8,128)S(1)}, f32[2,160,2432]{2,1,0:T(8,128)}, u32[]{:S(2)}) copy-start(f32[2,160,2432]{2,1,0:T(8,128)} %param.19) | copy-start | bytes 9338884
  474.9 8.1 %copy-start.1 = (f32[2,160,2432]{2,1,0:T(8,128)S(1)}, f32[2,160,2432]{2,1,0:T(8,128)}, u32[]{:S(2)}) copy-start(f32[2,160,2432]{2,1,0:T(8,128)} %param.16) | copy-start | bytes 9338884
  474.9 9.2 %copy-start.2 = (f32[2,160,2432]{2,1,0:T(8,128)S(1)}, f32[2,160,2432]{2,1,0:T(8,128)}, u32[]{:S(2)}) copy-start(f32[2,160,2432]{2,1,0:T(8,128)} %param.20) | copy-start | bytes 9338884
  474.9 10.1 %copy-start.3 = (f32[2,160,2432]{2,1,0:T(8,128)S(1)}, f32[2,160,2432]{2,1,0:T(8,128)}, u32[]{:S(2)}) copy-start(f32[2,160,2432]{2,1,0:T(8,128)} %param.17) | copy-start | bytes 9338884
  474.9 10.5 %copy-start.4 = (bf16[2,160,2432]{2,1,0:T(8,128)(2,1)S(1)}, bf16[2,160,2432]{2,1,0:T(8,128)(2,1)}, u32[]{:S(2)}) copy-start(bf16[2,160,2432]{2,1,0:T(8,128)(2,1)} %wg_ref.1) | copy-start | bytes 4669444
  474.9 10.9 %copy-start.5 = (bf16[2,160,2432]{2,1,0:T(8,128)(2,1)S(1)}, bf16[2,160,2432]{2,1,0:T(8,128)(2,1)}, u32[]{:S(2)}) copy-start(bf16[2,160,2432]{2,1,0:T(8,128)(2,1)} %wu_ref.1) | copy-start | bytes 4669444
  474.9 11.0 %copy-start.6 = (bf16[4,40,2432]{2,1,0:T(8,128)(2,1)S(1)}, bf16[4,40,2432]{2,1,0:T(8,128)(2,1)}, u32[]{:S(2)}) copy-start(bf16[4,40,2432]{2,1,0:T(8,128)(2,1)} %get-tuple-element.54) | copy-start | bytes 2334724
  474.9 11.2 %copy-start.7 = (bf16[4,40,2432]{2,1,0:T(8,128)(2,1)S(1)}, bf16[4,40,2432]{2,1,0:T(8,128)(2,1)}, u32[]{:S(2)}) copy-start(bf16[4,40,2432]{2,1,0:T(8,128)(2,1)} %get-tuple-element.58) | copy-start | bytes 2334724

commit v2 on v1

--- a/solution.py
+++ b/solution.py
@@ -8,6 +8,7 @@
 from jax.sharding import PartitionSpec as P
 
 F32, BF16 = jnp.float32, jnp.bfloat16
+HIDDEN_TILE = 512
 TILE = 512
 VMEM_LIMIT = 62 * 1024 * 1024
 
@@ -26,6 +27,10 @@
 
 def rows(tile, width):
     return pl.BlockSpec((tile, width), lambda i: (i, 0))
+
+
+def columns(height, tile):
+    return pl.BlockSpec((height, tile), lambda i: (0, i))
 
 
 def whole(*shape):
@@ -125,7 +130,7 @@
             one.wait_send()
 
 
-def forward_body(x_ref, wg_ref, wu_ref, wd_ref, a_ref, g_ref, u_ref, h_ref, a1_ref, d0_ref, g1_ref, u1_ref, d1_ref, *scratch):
+def forward_body(x_ref, wg_ref, wu_ref, wd_ref, g_ref, u_ref, h_ref, a1_ref, across_ref, across1_ref, d0_ref, g1_ref, u1_ref, d1_ref, *scratch):
     fulls, (z_ref, send, recv, local) = scratch[:6], scratch[6:]
     i = pl.program_id(0)
     place = Place()
@@ -157,7 +162,7 @@
             one.last()
 
     a = norm_of(x_ref[...])
-    a_ref[...] = a
+    across_ref[...] = a.T
     for at, n in cuts(z_ref.shape[1]):
         at = slice(at, at + n)
         g = dot(a, fulls[0][:, at])
@@ -167,7 +172,9 @@
         z_ref[:, at] = (silu_parts(g)[1] * u).astype(BF16)
     h = (x_ref[...].astype(F32) + dot(z_ref[...], fulls[2][...]).astype(BF16).astype(F32)).astype(BF16)
     h_ref[...] = h
-    a1_ref[...] = norm_of(h)
+    a1 = norm_of(h)
+    a1_ref[...] = a1
+    across1_ref[...] = a1.T
 
     @pl.when(i == pl.num_programs(0) - 1)
     def _():
@@ -189,8 +196,8 @@
         forward_body,
         grid=(t // tile,),
         in_specs=[rows(tile, d), ANY, ANY, ANY],
-        out_specs=[rows(tile, d), rows(tile, f), rows(tile, f), rows(tile, d), rows(tile, d)] + [ANY] * 4,
-        out_shape=[sds((t, d), BF16), sds((t, f), F32), sds((t, f), F32), sds((t, d), BF16), sds((t, d), BF16)]
+        out_specs=[rows(tile, f), rows(tile, f), rows(tile, d), rows(tile, d), columns(d, tile), columns(d, tile)] + [ANY] * 4,
+        out_shape=[sds((t, f), F32), sds((t, f), F32), sds((t, d), BF16), sds((t, d), BF16), sds((d, t), BF16), sds((d, t), BF16)]
         + [sds(one, BF16) for one in mats[2:]],
         scratch_shapes=[pltpu.VMEM(one, BF16) for one in mats] + [pltpu.VMEM((tile, f), BF16), DMA((6, 5)), DMA((6, 5)), DMA((6,))],
         compiler_params=pltpu.CompilerParams(
@@ -204,7 +211,7 @@
 class Sum:
     def __init__(self, place, term, out, squares, buffers, sems):
         self.p, self.term, self.out, self.squares = place, term, out, squares
-        self.rc, self.rx, self.sx, self.keep, self.ry, self.ra, self.rb, self.fin, self.temp = buffers
+        self.rc, self.rx, self.sx, self.keep, self.ry, self.ra, self.rb, self.fin = buffers
         send, recv, self.local = sems
         p = place
         self.ka, self.kx = [], None
@@ -222,43 +229,39 @@
         self.wide = p.copy(half, half, send.at[7], recv.at[7], "y")
         self.done = pltpu.make_async_copy(self.fin, out, self.local.at[0])
 
+    def loads(self):
+        p = self.p
+        return [
+            pltpu.make_async_copy(self.term.at[pl.ds(4 * (2 * x + p.c), 4)], to, self.local.at[k])
+            for k, (x, to) in enumerate(((1 - p.x, self.sx), (p.x, self.fin)))
+        ]
+
     def a(self):
-        for one in self.ka:
+        for one in self.ka + self.loads():
             one.start()
 
     def b(self):
         p = self.p
         for one in self.ka:
             one.wait_recv()
-        loads = []
-        for k, x in enumerate((1 - p.x, p.x)):
-            loads.append(pltpu.make_async_copy(self.term.at[pl.ds(4 * (2 * x + p.c), 4)], self.temp.at[2 * k], self.local.at[2 * k]))
-            loads.append(pltpu.make_async_copy(self.rc.at[x], self.temp.at[2 * k + 1], self.local.at[2 * k + 1]))
-        for one in loads:
-            one.start()
-        for one in loads[:2]:
+        for one in self.loads():
             one.wait()
         for q in range(4):
-            self.sx[q] = (self.temp[0, q].astype(F32) + self.temp[1, q].astype(F32)).astype(BF16)
+            self.sx[q] = (self.sx[q].astype(F32) + self.rc[1 - p.x, q].astype(F32)).astype(BF16)
         self.cx.start()
-        for one in loads[2:]:
-            one.wait()
         for q in range(4):
-            self.keep[q] = self.temp[2, q].astype(F32) + self.temp[3, q].astype(F32)
+            self.keep[q] = self.fin[q].astype(F32) + self.rc[p.x, q].astype(F32)
 
     def c_(self):
         self.cx.wait()
-        load = pltpu.make_async_copy(self.rx, self.temp.at[0], self.local.at[0])
-        load.start()
-        load.wait()
         p = self.p
         for q in range(2):
             at = 2 * (1 - p.y) + q
-            self.sx[q] = (self.keep[at] + self.temp[0, at].astype(F32)).astype(BF16)
+            self.sx[q] = (self.keep[at] + self.rx[at].astype(F32)).astype(BF16)
         self.cy.start()
         for q in range(2):
             at = 2 * p.y + q
-            self.keep[at] = self.keep[at] + self.temp[0, at].astype(F32)
+            self.keep[at] = self.keep[at] + self.rx[at].astype(F32)
 
     def d(self):
         self.cy.wait_recv()
@@ -301,6 +304,8 @@
 def sum_scratch(shape):
     _, a, b = shape
     return [
+        pltpu.VMEM((2, 4, a, b), BF16),
+        pltpu.VMEM((4, a, b), BF16),
         pltpu.VMEM((4, a, b), BF16),
         pltpu.VMEM((4, a, b), F32),
         pltpu.VMEM((2, a, b), BF16),
@@ -310,10 +315,6 @@
     ]
 
 
-def landing(shape):
-    return [sds((2, 4) + shape[1:], BF16), sds((4,) + shape[1:], BF16)]
-
-
 def kept_out(shape):
     return sds((4,) + shape[1:], BF16)
 
@@ -322,7 +323,7 @@
     return [refs[at + k * per : at + (k + 1) * per] for k in range(count)]
 
 
-def make_sums(place, terms, outs, squares, lands, own, temps, sems):
+def make_sums(place, terms, outs, squares, own, sems):
     send, recv, local = sems
     return [
         Sum(
@@ -330,7 +331,7 @@
             terms[k],
             outs[k],
             squares,
-            (lands[k][0], lands[k][1], own[k][0], own[k][1], own[k][2], own[k][3], own[k][4], own[k][5], temps[terms[k].shape[2]]),
+            own[k],
             (send.at[k], recv.at[k], local.at[k]),
         )
         for k in range(len(terms))
@@ -367,92 +368,58 @@
         out[k] = acc[k * n : (k + 1) * n, :].astype(BF16)
 
 
-def hidden_body(a_ref, dy_ref, wg_ref, wu_ref, wd_ref, dg_ref, du_ref, dwd_ref, acc):
+def hidden_body(a_ref, dy_ref, across_ref, wg_ref, wu_ref, wd_ref, dg_ref, du_ref, dwg_ref, dwu_ref, dwd_ref, acc_g, acc_u, acc_d):
     i = pl.program_id(0)
 
     @pl.when(i == 0)
     def _():
-        acc[...] = jnp.zeros_like(acc)
-
-    a, dy = a_ref[...], dy_ref[...]
+        for acc in (acc_g, acc_u, acc_d):
+            acc[...] = jnp.zeros_like(acc)
+
+    a, dy, across_a = a_ref[...], dy_ref[...], across_ref[...]
     across = dy.T
-    for at, n in cuts(acc.shape[1]):
+    for at, n in cuts(acc_d.shape[1]):
         at = slice(at, at + n)
         g, u = dot(a, wg_ref[:, at]), dot(a, wu_ref[:, at])
         z, dg, du = algebra(g, u, dot(dy, wd_ref[at, :], 1, 1))
         dg_ref[:, at] = dg
         du_ref[:, at] = du
-        acc[:, at] += dot(across, z)
+        acc_d[:, at] += dot(across, z)
+        acc_g[:, at] += dot(across_a, dg)
+        acc_u[:, at] += dot(across_a, du)
 
     @pl.when(i == pl.num_programs(0) - 1)
     def _():
-        store_turned(dwd_ref, acc)
-
-
-def hidden(a, dy, wg, wu, wd):
+        store_quarters(dwg_ref, acc_g)
+        store_quarters(dwu_ref, acc_u)
+        store_turned(dwd_ref, acc_d)
+
+
+def hidden(a, dy, across, wg, wu, wd):
     t, d = dy.shape
     f = wd.shape[0]
-    tile = 512
-    shape = quarters((f, d))
+    tile = HIDDEN_TILE
+    shapes = [quarters((d, f)), quarters((d, f)), quarters((f, d))]
     return pl.pallas_call(
         hidden_body,
         grid=(t // tile,),
-        in_specs=[rows(tile, d), rows(tile, d), once(d, f), once(d, f), once(f, d)],
-        out_specs=[rows(tile, f), rows(tile, f), once(*shape)],
-        out_shape=[sds((t, f), BF16), sds((t, f), BF16), sds(shape, BF16)],
-        scratch_shapes=[pltpu.VMEM((d, f), F32)],
-        compiler_params=params("arbitrary"),
-        cost_estimate=cost(8 * t * d * f, 12 * t * f),
+        in_specs=[rows(tile, d), rows(tile, d), columns(d, tile), once(d, f), once(d, f), once(f, d)],
+        out_specs=[rows(tile, f), rows(tile, f)] + [once(*one) for one in shapes],
+        out_shape=[sds((t, f), BF16), sds((t, f), BF16)] + [sds(one, BF16) for one in shapes],
+        scratch_shapes=[pltpu.VMEM((d, f), F32)] * 3,
+        compiler_params=pltpu.CompilerParams(dimension_semantics=("arbitrary",), vmem_limit_bytes=67043328),
+        cost_estimate=cost(12 * t * d * f, 12 * t * f),
         name="hidden",
-    )(a, dy, wg, wu, wd)
-
-
-def grads_body(a_ref, c_ref, e_ref, out_c, out_e, acc_c, acc_e):
-    i = pl.program_id(0)
-
-    @pl.when(i == 0)
-    def _():
-        acc_c[...] = jnp.zeros_like(acc_c)
-        acc_e[...] = jnp.zeros_like(acc_e)
-
-    across = a_ref[...].T
-    for acc, ref in ((acc_c, c_ref), (acc_e, e_ref)):
-        for at, n in cuts(ref.shape[1]):
-            at = slice(at, at + n)
-            acc[:, at] += dot(across, ref[:, at])
-
-    @pl.when(i == pl.num_programs(0) - 1)
-    def _():
-        store_quarters(out_c, acc_c)
-        store_quarters(out_e, acc_e)
-
-
-def grads(a, c, e):
-    (t, d), f = a.shape, c.shape[1]
-    tile = 512
-    shape = quarters((d, f))
-    return pl.pallas_call(
-        grads_body,
-        grid=(t // tile,),
-        in_specs=[rows(tile, d), rows(tile, f), rows(tile, f)],
-        out_specs=[once(*shape)] * 2,
-        out_shape=[sds(shape, BF16)] * 2,
-        scratch_shapes=[pltpu.VMEM((d, f), F32)] * 2,
-        compiler_params=params("arbitrary"),
-        cost_estimate=cost(4 * t * d * f, 4 * t * f),
-        name="grads",
-    )(a, c, e)
+    )(a, dy, across, wg, wu, wd)
 
 
 def back_body(dg1, du1, h_ref, dy_ref, g_ref, u_ref, wg_ref, wu_ref, wd_ref, *refs):
     terms, refs = refs[:3], refs[3:]
     dg_ref, du_ref, dwd_ref, sq_ref = refs[:4]
-    outs, lands, refs = refs[4:7], [refs[7:9], refs[9:11], refs[11:13]], refs[13:]
-    acc, own, refs = refs[0], split_up(1, 6, refs), refs[19:]
-    temps = {terms[0].shape[2]: refs[0], terms[2].shape[2]: refs[1]}
+    outs, acc, own, sems = refs[4:7], refs[7], split_up(8, 8, refs), refs[32:]
     i = pl.program_id(0)
     place = Place()
-    sums = make_sums(place, terms, outs, sq_ref, lands, own, temps, refs[2:5])
+    sums = make_sums(place, terms, outs, sq_ref, own, sems)
 
     @pl.when(i == 0)
     def _():
@@ -462,7 +429,7 @@
             sums[k].a()
         acc[...] = jnp.zeros_like(acc)
 
-    plan = {1: ("b2", "b0", "b1"), 4: ("c2",), 6: ("d2", "c0"), 7: ("e2",), 8: ("d0", "f2", "c1"), 9: ("e0",), 10: ("g2", "d1", "f0"), 11: ("e1",), 12: ("h2", "g0", "f1"), 13: ("g1",), 14: ("h0",), 15: ("h1",)}
+    plan = {1: ("b2",), 2: ("b0",), 3: ("b1",), 5: ("c2",), 7: ("d2", "c0"), 8: ("e2",), 9: ("d0", "f2"), 10: ("c1", "e0"), 11: ("g2", "f0"), 12: ("d1",), 13: ("h2", "g0", "e1"), 14: ("f1",), 15: ("h0", "g1")}
     for at, what in plan.items():
 
         @pl.when(i == at)
@@ -489,6 +456,7 @@
     @pl.when(i == pl.num_programs(0) - 1)
     def _():
         store_turned(dwd_ref, acc)
+        stage(sums, "h1")
         for one in sums:
             one.finish()
 
@@ -499,18 +467,13 @@
 
 
 def sum_outs(shapes):
-    kinds = [kept_out(one) for one in shapes]
-    for one in shapes:
-        kinds += landing(one)
-    return kinds
+    return [kept_out(one) for one in shapes]
 
 
 def sum_own(shapes):
     out = []
     for one in shapes:
         out += sum_scratch(one)
-    for one in dict.fromkeys(shapes):
-        out.append(pltpu.VMEM((4, 4) + one[1:], BF16))
     n = len(shapes)
     return out + [DMA((n, 8)), DMA((n, 8)), DMA((n, 4))]
 
@@ -541,16 +504,17 @@
 
 
 def tail_body(a_ref, c_ref, e_ref, term_d, sq1_ref, *refs):
-    tot_ref, outs, lands, refs = refs[0], refs[1:5], split_up(5, 2, refs, 4), refs[13:]
-    sq_ref, acc, made, own, refs = refs[0], refs[1], refs[2:5], split_up(5, 6, refs, 4), refs[29:]
+    tot_ref, g_ref, u_ref, d_ref = refs[:4]
+    refs = refs[4:]
+    sq_ref, acc, made, own, refs = refs[0], refs[1], refs[2:5], split_up(5, 8, refs, 4), refs[37:]
     terms = (*made, term_d)
-    temps = {one.shape[2]: refs[k] for k, one in enumerate(terms)}
-    tot_in, tot_send, tot_recv = refs[7:10]
+    tot_in, tot_send, tot_recv = refs[3:6]
     i = pl.program_id(0)
     n = pl.num_programs(0) // 3
     cut = made[1].shape[2]
+    outs = (g_ref, u_ref.at[:, :, pl.ds(0, cut)], u_ref.at[:, :, pl.ds(cut, u_ref.shape[2] - cut)], d_ref)
     place = Place()
-    sums = make_sums(place, terms, outs, sq_ref, lands, own, temps, refs[4:7])
+    sums = make_sums(place, terms, outs, sq_ref, own, refs[:3])
 
     @pl.when(i == 0)
     def _():
@@ -562,7 +526,7 @@
     def _():
         acc[...] = jnp.zeros_like(acc)
 
-    plan = {1: ("b3",), 4: ("b0",), 5: ("c3",), 8: ("b1", "d3"), 9: ("c0", "e3"), 10: ("f3",), 11: ("g3", "d0")}
+    plan = {1: ("b3",), 5: ("b0", "c3"), 7: ("d3",), 8: ("e3",), 9: ("b1", "c0"), 10: ("f3", "d0"), 11: ("g3",)}
     for at, what in plan.items():
 
         @pl.when(i == at)
@@ -571,7 +535,7 @@
                 stage(sums, one)
 
     def add(ref, lo, hi):
-        across = a_ref[...].T
+        across = a_ref[...]
         for at in range(lo, hi, 256):
             at = slice(at, min(at + 256, hi))
             acc[:, at] += dot(across, ref[:, at])
@@ -608,19 +572,19 @@
 
 
 def tail(a, c, e, term_d, squares):
-    (t, d), f = a.shape, c.shape[1]
+    (d, t), f = a.shape, c.shape[1]
     tile = 1024
     n = t // tile
     cut = f // 256 // 2 * 256 + 256
     made = quarters((d, f))
     shapes = [made, made[:2] + (cut,), made[:2] + (f - cut,), term_d.shape]
-    kinds = sum_outs(shapes)
+    kinds = sum_outs([made, made, term_d.shape])
     smem = pl.BlockSpec(memory_space=pltpu.SMEM)
     results = pl.pallas_call(
         tail_body,
         grid=(3 * n,),
         in_specs=[
-            pl.BlockSpec((tile, d), lambda i: (i % n, 0)),
+            pl.BlockSpec((d, tile), lambda i: (0, i % n)),
             pl.BlockSpec((tile, f), lambda i: (jnp.minimum(i, n - 1), 0)),
             pl.BlockSpec((tile, f), lambda i: (jnp.where(i < n, 0, i % n), 0)),
             ANY,
@@ -638,19 +602,17 @@
         cost_estimate=cost(4 * t * d * f, 4 * t * f),
         name="tail",
     )(a, c, e, term_d, squares)
-    return results[0][0, 0], results[1:5]
+    return results[0][0, 0], results[1:4]
 
 
 def solution(mesh):
     def step(x, dy, *arrays):
         x, dy = x[0], dy[0]
         weights, m, v = (arrays[i : i + 3] for i in (0, 3, 6))
-        a0, g0, u0, h1, a1, wd0, wg1, wu1, wd1 = forward(x, *weights)
-        dg1, du1, d_wd1 = hidden(a1, dy, wg1, wu1, wd1)
-        d_wg1, d_wu1 = grads(a1, dg1, du1)
+        g0, u0, h1, a1, across0, across1, wd0, wg1, wu1, wd1 = forward(x, *weights)
+        dg1, du1, d_wg1, d_wu1, d_wd1 = hidden(a1, dy, across1, wg1, wu1, wd1)
         (dg0, du0, d_wd0), squares1, sums1 = back(dg1, du1, h1, dy, g0, u0, wg1, wu1, wd0, (d_wg1, d_wu1, d_wd1))
-        squares, (s_g, s_ua, s_ub, s_d) = tail(a0, dg0, du0, d_wd0, squares1)
-        sums0 = (s_g, jnp.concatenate([s_ua, s_ub], -1), s_d)
+        squares, sums0 = tail(across0, dg0, du0, d_wd0, squares1)
         count = 4 * sum(w.size for w in weights)
         factor = jnp.minimum(1.0, 0.5 * lax.rsqrt(squares / count + 1e-30))
         new = []

time: 503 us -> 472 us (0.938); the launches traced: 494 us -> 468 us
  Pallas kernels: 471 us -> 445 us
    pallas_call x2 -> x1, Pallas kernels: 159 us -> 105 us  [tail(): pl.pallas_call(tail_body, grid=(3 * n,), in_specs=[pl.BlockSpec((d, tile)...]
    pallas_call x1, Pallas kernels: 78.3 us -> 115 us  [hidden(): pl.pallas_call(hidden_body, grid=(t // tile,), in_specs=[rows(tile, d), r...]
    pallas_call x1, Pallas kernels: 127 us -> 117 us  [back(): pl.pallas_call(back_body, grid=(t // tile,), in_specs=[rows(tile, f), row...]
where the time goes in v2:
time: 472 us; the launch traced here: 468 us
  Pallas kernels  445 us (94%)
  other arithmetic  15.7 us (3%)
  local copies, waits for them, and re-layouts  5.16 us (1%)
    pallas_call x1, Pallas kernels, back(): pl.pallas_call(back_body, grid=(t // tile,), in_specs=[rows(tile, f), row...  117 us
    pallas_call x1, Pallas kernels, hidden(): pl.pallas_call(hidden_body, grid=(t // tile,), in_specs=[rows(tile, d), r...  115 us
    pallas_call x1, Pallas kernels, forward(): pl.pallas_call(forward_body, grid=(t // tile,), in_specs=[rows(tile, d),...  109 us
    pallas_call x1, Pallas kernels, tail(): pl.pallas_call(tail_body, grid=(3 * n,), in_specs=[pl.BlockSpec((d, tile)...  105 us
    convert_element_type x2, other arithmetic, step(): (w - 0.02 * (mi * lax.rsqrt(vi + 1e-08) + 0.1 * w)).astype(BF16)  15.7 us

profile of v2, /device:TPU:0, one launch (start us, length us, event | category | flops | bytes accessed | tf_op | source)
XLA Modules:
  0.0 468.1 jit_solution(4183455878400431807)
XLA Ops:
  0.6 108.6 %forward.1 = (f32[4096,2432]{1,0:T(8,128)}, f32[4096,2432]{1,0:T(8,128)}, bf16[4096,640]{1,0:T(8,128)(2,1)}, bf16[4096,640]{1,0:T(8,128)(2,1)}, bf16[640,4096]{1...) custom-call(bf16[4096,640]{1,0:T(8,128)(2,1)} %bitcast.15, ...), custom_call_target="tpu_custom_call" | custom-call | flops 38252052480 | bytes 119537664 | tf_op jit(solution)/shard_map/forward/pallas_call | solution.py:195
  109.3 115.3 %hidden.1 = (bf16[4096,2432]{1,0:T(8,128)(2,1)}, bf16[4096,2432]{1,0:T(8,128)(2,1)}, bf16[16,40,2432]{2,1,0:T(8,128)(2,1)}, bf16[16,40,2432]{2,1,0:T(8,128)(2,1)}, bf16[16,152,640]{2,1,0:T(8,128)(2,1)}) custom-call(bf16[4096,640]{1,0:T(8,128)(2,1)} %get-tuple-element.36.a_ref, bf16[4096,640]{1,0:T(8,128)(2,1)} %bitcast.16, ...), custom_call_target="tpu_custom_call" | custom-call | flops 76504104960 | bytes 119537664 | tf_op jit(solution)/shard_map/hidden/pallas_call | solution.py:403
  224.6 116.6 %back.1 = (bf16[4096,2432]{1,0:T(8,128)(2,1)}, bf16[4096,2432]{1,0:T(8,128)(2,1)}, bf16[16,152,640]{2,1,0:T(8,128)(2,1)}, f32[1,1]{1,0:T(1,128)}, bf16[4,40,2432...) custom-call(bf16[4096,2432]{1,0:T(8,128)(2,1)} %get-tuple-element.41.dg1, ...), custom_call_target="tpu_custom_call" | custom-call | flops 51002736640 | bytes 119537664 | tf_op jit(solution)/shard_map/back/pallas_call | solution.py:488
  341.2 104.8 %tail.1 = (f32[8,128]{1,0:T(8,128)}, bf16[4,40,2432]{2,1,0:T(8,128)(2,1)}, bf16[4,40,2432]{2,1,0:T(8,128)(2,1)}, bf16[4,152,640]{2,1,0:T(8,128)(2,1)}) custom-call(bf16[640,4096]{1,0:T(8,128)(2,1)} %get-tuple-element.35.a_ref, bf16[4096,2432]{1,0:T(8,128)(2,1)} %get-tuple-element.50.c_ref, bf16[4096,2432]{1,0:T(8,128)(2,1)} %get-tuple-element.51.e_ref, ...), custom_call_target="tpu_custom_call" | custom-call | flops 25501368320 | bytes 39845888 | tf_op jit(solution)/shard_map/tail/pallas_call | solution.py:583
  446.0 1.2 slice.3
  447.9 0.0 copy-start
  447.9 0.0 copy-start.1
  447.9 0.0 copy-start.2
  447.9 0.0 copy-start.3
  447.9 0.0 copy-start.4
  448.0 0.0 copy-start.5
  448.0 0.0 copy-start.6
  448.0 0.0 copy-start.7
  448.0 7.3 %fusion.8 = (bf16[2,608,640]{2,1,0:T(8,128)(2,1)}, f32[2,608,640]{2,1,0:T(8,128)}, f32[2,608,640]{2,1,0:T(8,128)}) fusion(bf16[2,608,640]{2,1,0:T(8,128)(2,1)} %wd_ref.1, f32[]{:T(128)} %bitcast.4, bf16[1,608,640]{2,1,0:T(8,128)(2,1)} %bitcast.11, bf16[1,608,640]{2,1,0:T(8,128)(2,1)} %bitcast.14, f32[2,608,640]{2,1,0:T(8,128)} %param.21, ...), kind=kLoop, calls=%fused_computation.17 | loop fusion | flops 15564800 | bytes 17121284 | tf_op jit(solution)/shard_map/convert_element_type | solution.py:624
  455.3 0.0 copy-done
  455.3 0.8 copy-done.1
  456.1 1.1 copy-done.2
  457.1 0.9 copy-done.3
  458.0 0.4 copy-done.4
  458.4 0.4 copy-done.5
  458.9 0.2 copy-done.6
  459.0 0.2 copy-done.7
  459.2 8.4 %fusion.2 = (bf16[2,160,2432]{2,1,0:T(8,128)(2,1)}, f32[2,160,2432]{2,1,0:T(8,128)}, f32[2,160,2432]{2,1,0:T(8,128)}, bf16[2,160,2432]{2,1,0:T(8,128)(2,1)}, f32...) fusion(bf16[2,160,2432]{2,1,0:T(8,128)(2,1)S(1)} %copy-done.4, f32[]{:T(128)} %bitcast.4, ...), kind=kLoop, calls=%fused_computation.11 | loop fusion | flops 31129600 | bytes 34242564 | tf_op jit(solution)/shard_map/convert_element_type | solution.py:624
Async XLA Ops:
  447.9 7.4 %copy-start = (f32[2,160,2432]{2,1,0:T(8,128)S(1)}, f32[2,160,2432]{2,1,0:T(8,128)}, u32[]{:S(2)}) copy-start(f32[2,160,2432]{2,1,0:T(8,128)} %param.19) | copy-start | bytes 9338884
  447.9 8.2 %copy-start.1 = (f32[2,160,2432]{2,1,0:T(8,128)S(1)}, f32[2,160,2432]{2,1,0:T(8,128)}, u32[]{:S(2)}) copy-start(f32[2,160,2432]{2,1,0:T(8,128)} %param.16) | copy-start | bytes 9338884
  447.9 9.2 %copy-start.2 = (f32[2,160,2432]{2,1,0:T(8,128)S(1)}, f32[2,160,2432]{2,1,0:T(8,128)}, u32[]{:S(2)}) copy-start(f32[2,160,2432]{2,1,0:T(8,128)} %param.20) | copy-start | bytes 9338884
  447.9 10.1 %copy-start.3 = (f32[2,160,2432]{2,1,0:T(8,128)S(1)}, f32[2,160,2432]{2,1,0:T(8,128)}, u32[]{:S(2)}) copy-start(f32[2,160,2432]{2,1,0:T(8,128)} %param.17) | copy-start | bytes 9338884
  447.9 10.5 %copy-start.4 = (bf16[2,160,2432]{2,1,0:T(8,128)(2,1)S(1)}, bf16[2,160,2432]{2,1,0:T(8,128)(2,1)}, u32[]{:S(2)}) copy-start(bf16[2,160,2432]{2,1,0:T(8,128)(2,1)} %wg_ref.1) | copy-start | bytes 4669444
  448.0 10.9 %copy-start.5 = (bf16[2,160,2432]{2,1,0:T(8,128)(2,1)S(1)}, bf16[2,160,2432]{2,1,0:T(8,128)(2,1)}, u32[]{:S(2)}) copy-start(bf16[2,160,2432]{2,1,0:T(8,128)(2,1)} %wu_ref.1) | copy-start | bytes 4669444
  448.0 11.0 %copy-start.6 = (bf16[4,40,2432]{2,1,0:T(8,128)(2,1)S(1)}, bf16[4,40,2432]{2,1,0:T(8,128)(2,1)}, u32[]{:S(2)}) copy-start(bf16[4,40,2432]{2,1,0:T(8,128)(2,1)} %get-tuple-element.55) | copy-start | bytes 2334724
  448.0 11.3 %copy-start.7 = (bf16[4,40,2432]{2,1,0:T(8,128)(2,1)S(1)}, bf16[4,40,2432]{2,1,0:T(8,128)(2,1)}, u32[]{:S(2)}) copy-start(bf16[4,40,2432]{2,1,0:T(8,128)(2,1)} %get-tuple-element.58) | copy-start | bytes 2334724
